TPU v7x, 32 devices: a whole 2x2x4 slice. The times are simulated.
32 devices in a mesh: dp: 8 (over z, y), mp: 4 (over x, core).
Axes of the slice: x: 2, y: 2, z: 4, core: 2. Of those that a mesh axis runs over, the one named last changes fastest.
Arguments:
- hidden_input: bfloat16 [8192, 24], P('dp'), may hold values from -6 to 6
- output_cotangent: bfloat16 [8192, 8192], P('dp', 'mp'), may hold values from -0.023925781 to 0.023925781
- master_weights: float32 [24, 8192], P('dp', 'mp'), may hold values from -6 to 6
- first_codes: int32 [24, 8192], P('dp', 'mp'), may hold values from 0 to 15
- second_codes: int32 [24, 8192], P('dp', 'mp'), may hold values from 0 to 15
- first_rows: float32 [24], P('dp'), may hold values from 0.001 to 0.03
- first_cols: float32 [8192], P('mp'), may hold values from 0.001 to 0.03
- second_rows: float32 [24], P('dp'), may hold values from 1e-05 to 0.001
- second_cols: float32 [8192], P('mp'), may hold values from 1e-05 to 0.001
- step_count: int32 [], replicated, may hold values from 1 to 9
Outputs:
- new_master: float32 [24, 8192], P('dp', 'mp')
- update_ratio: float32 [24, 8192], P('dp', 'mp')
- gathered_params: bfloat16 [24, 8192], P(None, 'mp')
- first_scaled: float32 [24, 8192], P('dp', 'mp')
- second_scaled: float32 [24, 8192], P('dp', 'mp')
- new_first_rows: float32 [24], P('dp')
- new_first_cols: float32 [8192], P('mp')
- new_second_rows: float32 [24], P('dp')
- new_second_cols: float32 [8192], P('mp')
All inputs are finite; a program needn't handle non-finite values.
Results may differ from a plain program's by a relative error of at most 0.001.
Values may be sent and summed in bfloat16 or wider, within the bound.
A program may use at most 64 MiB of HBM per device.

v0:
```python
import jax
import jax.numpy as jnp
from jax import lax
from jax.sharding import PartitionSpec as P


def shards(
    hidden_input,
    output_cotangent,
    master_weights,
    first_codes,
    second_codes,
    first_rows,
    first_cols,
    second_rows,
    second_cols,
    step_count,
):
    local_rows = master_weights.shape[0]
    local_cols = master_weights.shape[1]
    whole_term = jnp.dot(hidden_input.T, output_cotangent, preferred_element_type=jnp.float32)
    column_share = lax.psum_scatter(whole_term, "dp", scatter_dimension=1, tiled=True)
    gradient = lax.all_to_all(column_share, "dp", split_axis=0, concat_axis=1, tiled=True)
    squares = lax.psum(jnp.sum(gradient * gradient), ("dp", "mp"))
    entries = local_rows * local_cols * lax.axis_size("dp") * lax.axis_size("mp")
    clipf = jnp.minimum(1.0, 0.01 * jnp.sqrt(jnp.float32(entries)) / (jnp.sqrt(squares) + 1e-06))
    clipped = clipf * gradient
    first_old = (
        (first_codes.astype(jnp.float32) - 7.5)
        / 7.5
        * jnp.minimum(first_rows[:, None], first_cols[None, :])
    )
    second_level = (second_codes.astype(jnp.float32) + 1.0) / 16.0
    second_old = (
        second_level * second_level * jnp.minimum(second_rows[:, None], second_cols[None, :])
    )
    first_new = 0.9 * first_old + 0.1 * clipped
    second_new = 0.95 * second_old + 0.05 * clipped * clipped
    steps = step_count.astype(jnp.float32)
    first_fix = 1.0 - jnp.power(jnp.float32(0.9), steps)
    second_fix = 1.0 - jnp.power(jnp.float32(0.95), steps)
    update_ratio = first_new / first_fix / (jnp.sqrt(second_new / second_fix) + 1e-08)
    new_master = master_weights - 0.001 * (update_ratio + 0.1 * master_weights)
    gathered_params = lax.all_gather(new_master.astype(jnp.bfloat16), "dp", axis=0, tiled=True)
    first_abs = jnp.abs(first_new)
    first_rowpart = jnp.max(first_abs, axis=1)
    first_colpart = jnp.max(first_abs, axis=0)
    second_rowpart = jnp.max(second_new, axis=1)
    second_colpart = jnp.max(second_new, axis=0)
    new_first_rows, new_second_rows = lax.pmax((first_rowpart, second_rowpart), "mp")
    new_first_cols, new_second_cols = lax.pmax((first_colpart, second_colpart), "dp")
    first_scaled = first_new / (
        jnp.minimum(new_first_rows[:, None], new_first_cols[None, :]) + 1e-08
    )
    second_scaled = second_new / (
        jnp.minimum(new_second_rows[:, None], new_second_cols[None, :]) + 1e-08
    )
    return (
        new_master,
        update_ratio,
        gathered_params,
        first_scaled,
        second_scaled,
        new_first_rows,
        new_first_cols,
        new_second_rows,
        new_second_cols,
    )


def solution(mesh):
    return jax.shard_map(
        shards,
        mesh=mesh,
        in_specs=(
            P("dp", None),
            P("dp", "mp"),
            P("dp", "mp"),
            P("dp", "mp"),
            P("dp", "mp"),
            P("dp"),
            P("mp"),
            P("dp"),
            P("mp"),
            P(),
        ),
        out_specs=(
            P("dp", "mp"),
            P("dp", "mp"),
            P(None, "mp"),
            P("dp", "mp"),
            P("dp", "mp"),
            P("dp"),
            P("mp"),
            P("dp"),
            P("mp"),
        ),
        check_vma=False,
    )
```

profile of v0, /device:TPU:0, one launch (start us, length us, event | category | flops | bytes accessed | tf_op | source)
XLA Modules:
  0.0 209.0 jit_solution(5620528497959128077)
XLA Ops:
  7.2 0.0 copy-start
  7.2 0.0 copy-start.4
  7.2 0.0 copy-start.8
  7.2 0.0 copy-start.5
  7.2 0.0 copy-start.9
  7.2 0.0 copy-start.1
  7.2 0.0 copy-start.2
  7.3 0.0 copy-start.3
  7.3 0.0 reduce-scatter.2.cloned.1.call-start
  7.3 0.7 copy-done
  8.0 3.5 %fusion.3 = f32[24,2048]{1,0:T(8,128)} fusion(bf16[1024,24]{0,1:T(8,128)(2,1)S(1)} %copy-done, bf16[1024,2048]{1,0:T(8,128)(2,1)} %param.11), kind=kOutput, calls=%fused_computation.13 | convolution fusion | flops 100663296 | bytes 4440064 | tf_op jit(solution)/shard_map/dot_general | solution.py:21
  11.5 0.0 reduce-scatter.2.cloned.1.call-update
  11.5 64.8 %reduce-scatter.2.cloned.1.call-done = f32[24,256]{1,0:T(8,128)} async-done(((f32[24,2048]{1,0:T(8,128)}), f32[24,256]{1,0:T(8,128)}) %reduce-scatter.2.cloned.1.call-update) | async-done | bytes 24592 | tf_op jit(solution)/shard_map/reduce_scatter | solution.py:22
  76.4 1.4 all_to_all.10
  77.7 3.6 %all-to-all-start = ((f32[8,3,256]{2,1,0:T(4,128)}), f32[8,3,256]{2,1,0:T(4,128)S(1)}, u32[]{:S(2)}, u32[]{:S(2)}) async-start(f32[8,3,256]{2,1,0:T(4,128)} %all_to_all.10), calls=%async_computation.1 | async-start | bytes 65536 | tf_op jit(solution)/shard_map/all_to_all | solution.py:23
  82.1 6.0 %all-to-all-done = f32[8,3,256]{2,1,0:T(4,128)S(1)} async-done(((f32[8,3,256]{2,1,0:T(4,128)}), f32[8,3,256]{2,1,0:T(4,128)S(1)}, u32[]{:S(2)}, u32[]{:S(2)}) %all-to-all-start) | async-done | bytes 24608 | tf_op jit(solution)/shard_map/all_to_all | solution.py:23
  88.0 0.6 multiply_reduce_fusion
  88.7 38.5 %psum.7 = f32[]{:T(128)} all-reduce(f32[]{:T(128)} %multiply_reduce_fusion), channel_id=1, replica_groups=mesh['dp'=8,'mp'=4] {'dp','mp'}, use_global_device_ids=true, to_apply=%region_2.0 | all-reduce | flops 1 | bytes 8 | tf_op jit(solution)/shard_map/psum | solution.py:24
  127.9 0.0 copy-done.4
  127.9 0.0 copy-done.8
  127.9 0.0 copy-done.5
  127.9 0.0 copy-done.9
  127.9 0.0 copy-done.1
  127.9 0.0 copy-done.2
  127.9 0.2 fusion.1
  128.2 6.5 %all-reduce.1 = (f32[3]{0:T(128)S(1)}, f32[3]{0:T(128)S(1)}) all-reduce(f32[3]{0:T(128)S(1)} %get-tuple-element.25, f32[3]{0:T(128)S(1)} %get-tuple-element.9), channel_id=1, replica_groups=mesh['dp'=8,'mp'=4] {'mp'}, use_global_device_ids=true, to_apply=%region_4.0 | all-reduce | flops 6 | bytes 48 | tf_op jit(solution)/shard_map/pmax | solution.py:50
  134.7 0.0 copy-start.10
  134.7 0.0 copy-start.11
  134.7 35.4 %all-reduce = (f32[2048]{0:T(1024)S(1)}, f32[2048]{0:T(1024)S(1)}) all-reduce(f32[2048]{0:T(1024)S(1)} %get-tuple-element.24, f32[2048]{0:T(1024)S(1)} %get-tuple-element.10), channel_id=1, replica_groups=mesh['dp'=8,'mp'=4] {'dp'}, use_global_device_ids=true, to_apply=%region_6.0 | all-reduce | flops 4096 | bytes 32768 | tf_op jit(solution)/shard_map/pmax | solution.py:51
  170.1 0.0 copy-start.6
  170.1 0.0 copy-start.7
  170.1 0.0 copy-done.3
  170.1 0.7 convert_bitcast_fusion
  170.9 30.5 %all-gather = bf16[8,3,2048]{2,1,0:T(4,128)(2,1)S(1)} all-gather(bf16[1,3,2048]{2,1,0:T(4,128)(2,1)S(1)} %get-tuple-element.19), channel_id=1, replica_groups=mesh['dp'=8,'mp'=4] {'dp'}, dimensions={0}, use_global_device_ids=true | all-gather | bytes 110592 | tf_op jit(solution)/shard_map/all_gather | solution.py:44
  201.4 0.7 reshape.32
  202.1 0.0 copy-done.10
  202.1 0.0 copy-done.11
  202.1 0.0 copy-done.6
  202.1 0.0 copy-done.7
  (1 shorter events, 0.0 us)
Async XLA Ops:
  7.2 0.8 copy-start
  7.2 120.7 %copy-start.4 = (f32[2048]{0:T(1024)S(1)}, f32[2048]{0:T(1024)}, u32[]{:S(2)}) copy-start(f32[2048]{0:T(1024)} %param.18) | copy-start | bytes 24580
  7.2 120.7 %copy-start.8 = (f32[3]{0:T(128)S(1)}, f32[3]{0:T(128)}, u32[]{:S(2)}) copy-start(f32[3]{0:T(128)} %param.17) | copy-start | bytes 40
  7.2 120.7 %copy-start.5 = (f32[2048]{0:T(1024)S(1)}, f32[2048]{0:T(1024)}, u32[]{:S(2)}) copy-start(f32[2048]{0:T(1024)} %param.16) | copy-start | bytes 24580
  7.2 120.7 %copy-start.9 = (f32[3]{0:T(128)S(1)}, f32[3]{0:T(128)}, u32[]{:S(2)}) copy-start(f32[3]{0:T(128)} %param.15) | copy-start | bytes 40
  7.2 120.7 %copy-start.1 = (s32[3,2048]{1,0:T(4,128)S(1)}, s32[3,2048]{1,0:T(4,128)}, u32[]{:S(2)}) copy-start(s32[3,2048]{1,0:T(4,128)} %param.14) | copy-start | bytes 73732
  7.2 120.7 %copy-start.2 = (s32[3,2048]{1,0:T(4,128)S(1)}, s32[3,2048]{1,0:T(4,128)}, u32[]{:S(2)}) copy-start(s32[3,2048]{1,0:T(4,128)} %param.13) | copy-start | bytes 73732
  7.3 162.9 %copy-start.3 = (f32[3,2048]{1,0:T(4,128)S(1)}, f32[3,2048]{1,0:T(4,128)}, u32[]{:S(2)}) copy-start(f32[3,2048]{1,0:T(4,128)} %param.12) | copy-start | bytes 73732
  7.3 69.1 %reduce-scatter.2.cloned.1.call-start = ((), (), s32[]{:S(2)}) async-start(), calls=%async_computation.2 | async-start | bytes 221184 | tf_op jit(solution)/shard_map/reduce_scatter | solution.py:22
  77.7 10.3 %all-to-all-start = ((f32[8,3,256]{2,1,0:T(4,128)}), f32[8,3,256]{2,1,0:T(4,128)S(1)}, u32[]{:S(2)}, u32[]{:S(2)}) async-start(f32[8,3,256]{2,1,0:T(4,128)} %all_to_all.10), calls=%async_computation.1 | async-start | bytes 65536 | tf_op jit(solution)/shard_map/all_to_all | solution.py:23
  134.7 67.4 %copy-start.10 = (f32[3]{0:T(128)}, f32[3]{0:T(128)S(1)}, u32[]{:S(2)}) copy-start(f32[3]{0:T(128)S(1)} %get-tuple-element.15) | copy-start | bytes 40
  134.7 67.4 %copy-start.11 = (f32[3]{0:T(128)}, f32[3]{0:T(128)S(1)}, u32[]{:S(2)}) copy-start(f32[3]{0:T(128)S(1)} %get-tuple-element.16) | copy-start | bytes 40
  170.1 32.0 %copy-start.6 = (f32[2048]{0:T(1024)}, f32[2048]{0:T(1024)S(1)}, u32[]{:S(2)}) copy-start(f32[2048]{0:T(1024)S(1)} %get-tuple-element.13) | copy-start | bytes 24580
  170.1 32.0 %copy-start.7 = (f32[2048]{0:T(1024)}, f32[2048]{0:T(1024)S(1)}, u32[]{:S(2)}) copy-start(f32[2048]{0:T(1024)S(1)} %get-tuple-element.14) | copy-start | bytes 24580
Sparse Core Ops, SparseCore 0:
  11.7 64.6 reduce-scatter.1
where the time goes:
time: 209 us
  blocking collectives  111 us (53%)
  waiting for transfers between devices  70.8 us (34%)
  between operations  15.7 us (8%)
  starting transfers between devices  3.65 us (2%)
  matrix products  3.52 us (2%)
  local copies, waits for them, and re-layouts  2.81 us (1%)
    reduce_scatter x1, waiting for transfers between devices, shards(): lax.psum_scatter(whole_term, 'dp', scatter_dimension=1, tiled=True)  64.8 us
    psum x1, blocking collectives, shards(): squares = lax.psum(jnp.sum(gradient * gradient), ('dp', 'mp'))  38.5 us
    pmax x1, blocking collectives, shards(): lax.pmax((first_colpart, second_colpart), 'dp')  35.4 us
    all_gather x1, blocking collectives, shards(): lax.all_gather(new_master.astype(jnp.bfloat16), 'dp', axis=0, tiled=True)  30.5 us
    pmax x1, blocking collectives, shards(): lax.pmax((first_rowpart, second_rowpart), 'mp')  6.54 us
    all_to_all x1, waiting for transfers between devices, shards(): lax.all_to_all(column_share, 'dp', split_axis=0, concat_axis=1, tiled=True)  5.95 us
  transfers between devices with their start and end apart: 2, of which 2 were waited for; matrix products, arithmetic and copies ran while one was open for 0% of the time, Pallas kernels for 0%

commit v1 on v0

--- a/solution.py
+++ b/solution.py
@@ -20,7 +20,10 @@
     local_cols = master_weights.shape[1]
     whole_term = jnp.dot(hidden_input.T, output_cotangent, preferred_element_type=jnp.float32)
     column_share = lax.psum_scatter(whole_term, "dp", scatter_dimension=1, tiled=True)
-    gradient = lax.all_to_all(column_share, "dp", split_axis=0, concat_axis=1, tiled=True)
+    gradient = jnp.concatenate(
+        lax.all_to_all(jnp.stack(jnp.split(column_share, lax.axis_size("dp"), axis=0)), "dp", 0, 0),
+        axis=1,
+    )
     squares = lax.psum(jnp.sum(gradient * gradient), ("dp", "mp"))
     entries = local_rows * local_cols * lax.axis_size("dp") * lax.axis_size("mp")
     clipf = jnp.minimum(1.0, 0.01 * jnp.sqrt(jnp.float32(entries)) / (jnp.sqrt(squares) + 1e-06))

time: 209 us -> 219 us (1.048)
  local copies, waits for them, and re-layouts: 2.81 us -> 11.8 us
    unnamed x25 -> x32, local copies, waits for them, and re-layouts: 1.45 us -> 10.5 us
where the time goes in v1:
time: 219 us; the launch traced here: 218 us
  blocking collectives  111 us (51%)
  waiting for transfers between devices  70.8 us (32%)
  between operations  15.7 us (7%)
  local copies, waits for them, and re-layouts  11.8 us (5%)
  starting transfers between devices  3.65 us (2%)
  matrix products  3.52 us (2%)
    reduce_scatter x1, waiting for transfers between devices, shards(): lax.psum_scatter(whole_term, 'dp', scatter_dimension=1, tiled=True)  64.8 us
    psum x1, blocking collectives, shards(): squares = lax.psum(jnp.sum(gradient * gradient), ('dp', 'mp'))  38.5 us
    pmax x1, blocking collectives, shards(): lax.pmax((first_colpart, second_colpart), 'dp')  35.4 us
    all_gather x1, blocking collectives, shards(): lax.all_gather(new_master.astype(jnp.bfloat16), 'dp', axis=0, tiled=True)  30.5 us
    unnamed x32, local copies, waits for them, and re-layouts  10.5 us
    pmax x1, blocking collectives, shards(): lax.pmax((first_rowpart, second_rowpart), 'mp')  6.54 us
    all_to_all x1, waiting for transfers between devices, shards(): lax.all_to_all(jnp.stack(jnp.split(column_share, lax.axis_size('dp'), axi...  5.95 us
  transfers between devices with their start and end apart: 2, of which 2 were waited for; matrix products, arithmetic and copies ran while one was open for 0% of the time, Pallas kernels for 0%

profile of v1, /device:TPU:0, one launch (start us, length us, event | category | flops | bytes accessed | tf_op | source)
XLA Modules:
  0.0 218.0 jit_solution(5725910481369507343)
XLA Ops:
  7.2 0.0 copy-start
  7.2 0.0 copy-start.4
  7.2 0.0 copy-start.8
  7.2 0.0 copy-start.5
  7.2 0.0 copy-start.9
  7.2 0.0 copy-start.1
  7.2 0.0 copy-start.2
  7.3 0.0 copy-start.3
  7.3 0.0 reduce-scatter.2.cloned.1.call-start
  7.3 0.7 copy-done
  8.0 3.5 %fusion.3 = f32[24,2048]{1,0:T(8,128)} fusion(bf16[1024,24]{0,1:T(8,128)(2,1)S(1)} %copy-done, bf16[1024,2048]{1,0:T(8,128)(2,1)} %param.11), kind=kOutput, calls=%fused_computation.29 | convolution fusion | flops 100663296 | bytes 4440064 | tf_op jit(solution)/shard_map/dot_general | solution.py:21
  11.5 0.0 reduce-scatter.2.cloned.1.call-update
  11.5 64.8 %reduce-scatter.2.cloned.1.call-done = f32[24,256]{1,0:T(8,128)} async-done(((f32[24,2048]{1,0:T(8,128)}), f32[24,256]{1,0:T(8,128)}) %reduce-scatter.2.cloned.1.call-update) | async-done | bytes 24592 | tf_op jit(solution)/shard_map/reduce_scatter | solution.py:22
  76.4 1.3 constant_dynamic-update-slice_fusion.7
  77.7 1.3 constant_dynamic-update-slice_fusion.6
  79.0 1.3 constant_dynamic-update-slice_fusion.5
  80.3 1.3 constant_dynamic-update-slice_fusion.4
  81.6 1.3 constant_dynamic-update-slice_fusion.3
  82.9 1.3 constant_dynamic-update-slice_fusion.2
  84.2 1.3 constant_dynamic-update-slice_fusion.1
  85.5 1.3 constant_dynamic-update-slice_fusion
  86.7 3.6 %all-to-all-start = ((f32[8,3,256]{2,1,0:T(4,128)}), f32[8,3,256]{2,1,0:T(4,128)S(1)}, u32[]{:S(2)}, u32[]{:S(2)}) async-start(f32[8,3,256]{2,1,0:T(4,128)} %constant_dynamic-update-slice_fusion), calls=%async_computation.1 | async-start | bytes 65536 | tf_op jit(solution)/shard_map/all_to_all | solution.py:24
  91.1 6.0 %all-to-all-done = f32[8,3,256]{2,1,0:T(4,128)S(1)} async-done(((f32[8,3,256]{2,1,0:T(4,128)}), f32[8,3,256]{2,1,0:T(4,128)S(1)}, u32[]{:S(2)}, u32[]{:S(2)}) %all-to-all-start) | async-done | bytes 24608 | tf_op jit(solution)/shard_map/all_to_all | solution.py:24
  97.0 0.6 multiply_reduce_fusion
  97.7 38.5 %psum.7 = f32[]{:T(128)} all-reduce(f32[]{:T(128)} %multiply_reduce_fusion), channel_id=1, replica_groups=mesh['dp'=8,'mp'=4] {'dp','mp'}, use_global_device_ids=true, to_apply=%region_2.0 | all-reduce | flops 1 | bytes 8 | tf_op jit(solution)/shard_map/psum | solution.py:27
  136.9 0.0 copy-done.4
  136.9 0.0 copy-done.8
  136.9 0.0 copy-done.5
  136.9 0.0 copy-done.9
  136.9 0.0 copy-done.1
  136.9 0.0 copy-done.2
  136.9 0.2 fusion.1
  137.2 6.5 %all-reduce.1 = (f32[3]{0:T(128)S(1)}, f32[3]{0:T(128)S(1)}) all-reduce(f32[3]{0:T(128)S(1)} %get-tuple-element.25, f32[3]{0:T(128)S(1)} %get-tuple-element.9), channel_id=1, replica_groups=mesh['dp'=8,'mp'=4] {'mp'}, use_global_device_ids=true, to_apply=%region_4.0 | all-reduce | flops 6 | bytes 48 | tf_op jit(solution)/shard_map/pmax | solution.py:53
  143.7 0.0 copy-start.10
  143.7 0.0 copy-start.11
  143.7 35.4 %all-reduce = (f32[2048]{0:T(1024)S(1)}, f32[2048]{0:T(1024)S(1)}) all-reduce(f32[2048]{0:T(1024)S(1)} %get-tuple-element.24, f32[2048]{0:T(1024)S(1)} %get-tuple-element.10), channel_id=1, replica_groups=mesh['dp'=8,'mp'=4] {'dp'}, use_global_device_ids=true, to_apply=%region_6.0 | all-reduce | flops 4096 | bytes 32768 | tf_op jit(solution)/shard_map/pmax | solution.py:54
  179.1 0.0 copy-start.6
  179.1 0.0 copy-start.7
  179.1 0.0 copy-done.3
  179.1 0.7 convert_bitcast_fusion
  179.9 30.5 %all-gather = bf16[8,3,2048]{2,1,0:T(4,128)(2,1)S(1)} all-gather(bf16[1,3,2048]{2,1,0:T(4,128)(2,1)S(1)} %get-tuple-element.19), channel_id=1, replica_groups=mesh['dp'=8,'mp'=4] {'dp'}, dimensions={0}, use_global_device_ids=true | all-gather | bytes 110592 | tf_op jit(solution)/shard_map/all_gather | solution.py:47
  210.4 0.7 reshape.31
  211.1 0.0 copy-done.10
  211.1 0.0 copy-done.11
  211.1 0.0 copy-done.6
  211.1 0.0 copy-done.7
  (1 shorter events, 0.0 us)
Async XLA Ops:
  7.2 0.8 copy-start
  7.2 129.7 %copy-start.4 = (f32[2048]{0:T(1024)S(1)}, f32[2048]{0:T(1024)}, u32[]{:S(2)}) copy-start(f32[2048]{0:T(1024)} %param.18) | copy-start | bytes 24580
  7.2 129.7 %copy-start.8 = (f32[3]{0:T(128)S(1)}, f32[3]{0:T(128)}, u32[]{:S(2)}) copy-start(f32[3]{0:T(128)} %param.17) | copy-start | bytes 40
  7.2 129.7 %copy-start.5 = (f32[2048]{0:T(1024)S(1)}, f32[2048]{0:T(1024)}, u32[]{:S(2)}) copy-start(f32[2048]{0:T(1024)} %param.16) | copy-start | bytes 24580
  7.2 129.7 %copy-start.9 = (f32[3]{0:T(128)S(1)}, f32[3]{0:T(128)}, u32[]{:S(2)}) copy-start(f32[3]{0:T(128)} %param.15) | copy-start | bytes 40
  7.2 129.7 %copy-start.1 = (s32[3,2048]{1,0:T(4,128)S(1)}, s32[3,2048]{1,0:T(4,128)}, u32[]{:S(2)}) copy-start(s32[3,2048]{1,0:T(4,128)} %param.14) | copy-start | bytes 73732
  7.2 129.7 %copy-start.2 = (s32[3,2048]{1,0:T(4,128)S(1)}, s32[3,2048]{1,0:T(4,128)}, u32[]{:S(2)}) copy-start(s32[3,2048]{1,0:T(4,128)} %param.13) | copy-start | bytes 73732
  7.3 171.9 %copy-start.3 = (f32[3,2048]{1,0:T(4,128)S(1)}, f32[3,2048]{1,0:T(4,128)}, u32[]{:S(2)}) copy-start(f32[3,2048]{1,0:T(4,128)} %param.12) | copy-start | bytes 73732
  7.3 69.1 %reduce-scatter.2.cloned.1.call-start = ((), (), s32[]{:S(2)}) async-start(), calls=%async_computation.2 | async-start | bytes 221184 | tf_op jit(solution)/shard_map/reduce_scatter | solution.py:22
  86.7 10.3 %all-to-all-start = ((f32[8,3,256]{2,1,0:T(4,128)}), f32[8,3,256]{2,1,0:T(4,128)S(1)}, u32[]{:S(2)}, u32[]{:S(2)}) async-start(f32[8,3,256]{2,1,0:T(4,128)} %constant_dynamic-update-slice_fusion), calls=%async_computation.1 | async-start | bytes 65536 | tf_op jit(solution)/shard_map/all_to_all | solution.py:24
  143.7 67.4 %copy-start.10 = (f32[3]{0:T(128)}, f32[3]{0:T(128)S(1)}, u32[]{:S(2)}) copy-start(f32[3]{0:T(128)S(1)} %get-tuple-element.15) | copy-start | bytes 40
  143.7 67.4 %copy-start.11 = (f32[3]{0:T(128)}, f32[3]{0:T(128)S(1)}, u32[]{:S(2)}) copy-start(f32[3]{0:T(128)S(1)} %get-tuple-element.16) | copy-start | bytes 40
  179.1 32.0 %copy-start.6 = (f32[2048]{0:T(1024)}, f32[2048]{0:T(1024)S(1)}, u32[]{:S(2)}) copy-start(f32[2048]{0:T(1024)S(1)} %get-tuple-element.13) | copy-start | bytes 24580
  179.1 32.0 %copy-start.7 = (f32[2048]{0:T(1024)}, f32[2048]{0:T(1024)S(1)}, u32[]{:S(2)}) copy-start(f32[2048]{0:T(1024)S(1)} %get-tuple-element.14) | copy-start | bytes 24580
Sparse Core Ops, SparseCore 0:
  11.7 64.6 reduce-scatter.1
